TPU v7x, 32 devices: a whole 2x2x4 slice. The times are simulated.
32 devices in a mesh: row: 8 (over y, x, core), col: 4 (over z).
Axes of the slice: x: 2, y: 2, z: 4, core: 2. Of those that a mesh axis runs over, the one named last changes fastest.
Arguments:
- density_start: float32 [512, 512], P('row', 'col'), may hold values from -0.5 to 1, as said below
- branches: int32 [6], replicated, may hold values from 0 to 1, as said below
Outputs:
- density: float32 [512, 512], P('row', 'col')
- occupations: float32 [6, 2], replicated
Inputs may be any that keep to these rules, and one draw needn't show every extreme that they name: density_start is symmetric with eigenvalues inside 0 to 1. `branches`: each entry is 0 or 1, and exactly 3 entries are 1.
All inputs are finite; a program needn't handle non-finite values.
Results may differ from a plain program's by a relative error of at most 0.0025.
Values may be sent and summed in bfloat16 or wider, within the bound.
A program may use at most 64 MiB of HBM per device.

v0:
```python
import jax
import jax.numpy as jnp
from jax import lax
from jax.sharding import PartitionSpec as P

ITERS = 6


def taken_in(shard, axis, dim, absorb, state):
    everything = jax.tree.map(lambda a: lax.all_gather(a, axis, axis=dim, tiled=True), shard)
    return absorb(state, everything, jnp.int32(0))


def local_trace(matrix_block, diagonal_mask):
    return jnp.sum(matrix_block * diagonal_mask)


def body(density_start, branches):
    rows_here, cols_here = density_start.shape
    row_first = lax.axis_index("row") * rows_here
    col_first = lax.axis_index("col") * cols_here
    row_ids = row_first + lax.broadcasted_iota(jnp.int32, (rows_here, cols_here), 0)
    col_ids = col_first + lax.broadcasted_iota(jnp.int32, (rows_here, cols_here), 1)
    diagonal_mask = (row_ids == col_ids).astype(jnp.float32)
    size_total = cols_here * lax.axis_size("col")
    density = density_start
    records = []
    for iteration in range(ITERS):
        narrow = density.astype(jnp.bfloat16)
        empty = jnp.zeros((rows_here, cols_here), jnp.float32)
        plain_local = local_trace(density, diagonal_mask)
        row_panel = lax.all_gather(narrow, "col", axis=1, tiled=True)

        def add_rows(accumulated, shard_piece, offset):
            panel_part = lax.dynamic_slice_in_dim(row_panel, offset, shard_piece.shape[0], 1)
            return accumulated + jnp.dot(
                panel_part, shard_piece, preferred_element_type=jnp.float32
            )

        square = taken_in(narrow, "row", 0, add_rows, empty)
        square_local = local_trace(square, diagonal_mask)
        branch_now = branches[iteration]
        records.append(jnp.stack([plain_local, square_local]))
        density = jnp.where(branch_now == 1, 2.0 * density - square, square)
    stacked = jnp.stack(records)
    stacked = lax.psum(stacked, ("row", "col"))
    occupations = stacked / size_total
    return (density, occupations)


def solution(mesh):
    in_specs = (P("row", "col"), P())
    out_specs = (P("row", "col"), P())
    return jax.shard_map(body, mesh=mesh, in_specs=in_specs, out_specs=out_specs, check_vma=False)
```

profile of v0, /device:TPU:0, one launch (start us, length us, event | category | flops | bytes accessed | tf_op | source)
XLA Modules:
  0.0 191.1 jit_solution(16147823306401190443)
XLA Ops:
  0.6 0.0 copy-start
  0.7 1.6 fusion.17
  6.1 0.0 copy-done
  6.1 15.0 %all_gather.36 = bf16[64,512]{1,0:T(8,128)(2,1)S(1)} all-gather(bf16[64,128]{1,0:T(8,128)(2,1)S(1)} %convert_element_type.19), channel_id=1, replica_groups=mesh['row'=8,'col'=4] {'col'}, dimensions={1}, use_global_device_ids=true | all-gather | bytes 81920 | tf_op jit(solution)/shard_map/all_gather | solution.py:32
  21.1 9.2 %all_gather.37 = bf16[512,128]{1,0:T(8,128)(2,1)S(1)} all-gather(bf16[64,128]{1,0:T(8,128)(2,1)S(1)} %convert_element_type.19), channel_id=1, replica_groups=mesh['row'=8,'col'=4] {'row'}, dimensions={0}, use_global_device_ids=true | all-gather | bytes 147456 | tf_op jit(solution)/shard_map/all_gather | solution.py:10
  30.3 0.2 fusion.16
  30.4 13.2 %all_gather.38 = bf16[64,512]{1,0:T(8,128)(2,1)S(1)} all-gather(bf16[64,128]{1,0:T(8,128)(2,1)S(1)} %get-tuple-element.24), channel_id=1, replica_groups=mesh['row'=8,'col'=4] {'col'}, dimensions={1}, use_global_device_ids=true | all-gather | bytes 81920 | tf_op jit(solution)/shard_map/all_gather | solution.py:32
  43.6 9.1 %all_gather.39 = bf16[512,128]{1,0:T(8,128)(2,1)S(1)} all-gather(bf16[64,128]{1,0:T(8,128)(2,1)S(1)} %get-tuple-element.24), channel_id=1, replica_groups=mesh['row'=8,'col'=4] {'row'}, dimensions={0}, use_global_device_ids=true | all-gather | bytes 147456 | tf_op jit(solution)/shard_map/all_gather | solution.py:10
  52.8 0.2 fusion.15
  52.9 13.2 %all_gather.40 = bf16[64,512]{1,0:T(8,128)(2,1)S(1)} all-gather(bf16[64,128]{1,0:T(8,128)(2,1)S(1)} %get-tuple-element.22), channel_id=1, replica_groups=mesh['row'=8,'col'=4] {'col'}, dimensions={1}, use_global_device_ids=true | all-gather | bytes 81920 | tf_op jit(solution)/shard_map/all_gather | solution.py:32
  66.2 8.2 %all_gather.41 = bf16[512,128]{1,0:T(8,128)(2,1)S(1)} all-gather(bf16[64,128]{1,0:T(8,128)(2,1)S(1)} %get-tuple-element.22), channel_id=1, replica_groups=mesh['row'=8,'col'=4] {'row'}, dimensions={0}, use_global_device_ids=true | all-gather | bytes 147456 | tf_op jit(solution)/shard_map/all_gather | solution.py:10
  74.4 0.2 fusion.14
  74.5 13.2 %all_gather.42 = bf16[64,512]{1,0:T(8,128)(2,1)S(1)} all-gather(bf16[64,128]{1,0:T(8,128)(2,1)S(1)} %get-tuple-element.20), channel_id=1, replica_groups=mesh['row'=8,'col'=4] {'col'}, dimensions={1}, use_global_device_ids=true | all-gather | bytes 81920 | tf_op jit(solution)/shard_map/all_gather | solution.py:32
  87.7 9.1 %all_gather.43 = bf16[512,128]{1,0:T(8,128)(2,1)S(1)} all-gather(bf16[64,128]{1,0:T(8,128)(2,1)S(1)} %get-tuple-element.20), channel_id=1, replica_groups=mesh['row'=8,'col'=4] {'row'}, dimensions={0}, use_global_device_ids=true | all-gather | bytes 147456 | tf_op jit(solution)/shard_map/all_gather | solution.py:10
  96.9 0.2 fusion.13
  97.0 13.2 %all_gather.44 = bf16[64,512]{1,0:T(8,128)(2,1)S(1)} all-gather(bf16[64,128]{1,0:T(8,128)(2,1)S(1)} %get-tuple-element.18), channel_id=1, replica_groups=mesh['row'=8,'col'=4] {'col'}, dimensions={1}, use_global_device_ids=true | all-gather | bytes 81920 | tf_op jit(solution)/shard_map/all_gather | solution.py:32
  110.3 8.2 %all_gather.45 = bf16[512,128]{1,0:T(8,128)(2,1)S(1)} all-gather(bf16[64,128]{1,0:T(8,128)(2,1)S(1)} %get-tuple-element.18), channel_id=1, replica_groups=mesh['row'=8,'col'=4] {'row'}, dimensions={0}, use_global_device_ids=true | all-gather | bytes 147456 | tf_op jit(solution)/shard_map/all_gather | solution.py:10
  118.5 0.2 fusion.12
  118.6 13.2 %all_gather.46 = bf16[64,512]{1,0:T(8,128)(2,1)S(1)} all-gather(bf16[64,128]{1,0:T(8,128)(2,1)S(1)} %get-tuple-element.16), channel_id=1, replica_groups=mesh['row'=8,'col'=4] {'col'}, dimensions={1}, use_global_device_ids=true | all-gather | bytes 81920 | tf_op jit(solution)/shard_map/all_gather | solution.py:32
  131.8 9.1 %all_gather.47 = bf16[512,128]{1,0:T(8,128)(2,1)S(1)} all-gather(bf16[64,128]{1,0:T(8,128)(2,1)S(1)} %get-tuple-element.16), channel_id=1, replica_groups=mesh['row'=8,'col'=4] {'row'}, dimensions={0}, use_global_device_ids=true | all-gather | bytes 147456 | tf_op jit(solution)/shard_map/all_gather | solution.py:10
  141.0 1.5 fusion.10
  142.5 1.3 maximum_bitcast_fusion.5
  143.8 0.1 copy.10
  143.8 1.3 maximum_bitcast_fusion.4
  145.2 0.1 copy.9
  145.3 1.3 maximum_bitcast_fusion.3
  146.6 0.1 copy.8
  146.7 1.3 maximum_bitcast_fusion.2
  148.0 0.1 copy.7
  148.1 1.3 maximum_bitcast_fusion.1
  149.4 0.1 copy.6
  149.5 1.3 maximum_bitcast_fusion
  150.8 0.1 copy.5
  150.9 0.1 stack.99
  151.0 39.5 %psum.7 = f32[6,2]{0,1:T(2,128)S(1)} all-reduce(f32[6,2]{0,1:T(2,128)S(1)} %stack.99), channel_id=1, replica_groups=mesh['row'=8,'col'=4] {'row','col'}, use_global_device_ids=true, to_apply=%region_12.13 | all-reduce | flops 12 | bytes 96 | tf_op jit(solution)/shard_map/psum | solution.py:46
  190.5 0.6 broadcast_multiply_fusion
  (3 shorter events, 0.0 us)
Async XLA Ops:
  0.6 5.5 %copy-start = (f32[64,128]{1,0:T(8,128)S(1)}, f32[64,128]{1,0:T(8,128)}, u32[]{:S(2)}) copy-start(f32[64,128]{1,0:T(8,128)} %param.2) | copy-start | bytes 98308
where the time goes:
time: 192 us; the launch traced here: 191 us
  blocking collectives  174 us (91%)
  other arithmetic  8.46 us (4%)
  between operations  4.56 us (2%)
  matrix products  2.26 us (1%)
  local copies, waits for them, and re-layouts  2.23 us (1%)
    all_gather x6, blocking collectives, body(): row_panel = lax.all_gather(narrow, 'col', axis=1, tiled=True)  81.1 us
    all_gather x6, blocking collectives, taken_in(): lax.all_gather(a, axis, axis=dim, tiled=True)  53 us
    psum x1, blocking collectives, body(): stacked = lax.psum(stacked, ('row', 'col'))  39.5 us
    another operation x6, other arithmetic, body(): stacked = jnp.stack(records)  7.88 us

commit v1 on v0

v1 whole, which is shorter than its diff:
```python
import functools

import jax
import jax.numpy as jnp
from jax import lax
from jax.experimental import pallas as pl
from jax.experimental.pallas import tpu as pltpu
from jax.sharding import PartitionSpec as P

ITERS = 6


def diagonal_sum(square, first):
    rows, cols = square.shape
    row_ids = lax.broadcasted_iota(jnp.int32, (rows, cols), 0)
    col_ids = lax.broadcasted_iota(jnp.int32, (rows, cols), 1)
    return jnp.sum(jnp.where(row_ids == col_ids + first, square, 0.0), keepdims=True)


def purify(x, b, branches, rows_here, cols_here, density_ref, occupations_ref):
    size = x.shape[0]
    tile = min(256, size)
    tiles = size // tile
    row_first = pl.multiple_of(lax.axis_index("row") * rows_here, rows_here)
    col_first = pl.multiple_of(lax.axis_index("col") * cols_here, cols_here)
    trace = jnp.zeros((1, 1), jnp.float32)
    for t in range(tiles):
        ids = slice(t * tile, (t + 1) * tile)
        trace = trace + diagonal_sum(x[ids, ids], 0)
        b[0, :, ids] = x[:, ids].astype(jnp.bfloat16)
    records = []
    for iteration in range(ITERS):
        now, later = iteration % 2, (iteration + 1) % 2
        one = branches[iteration] == 1
        keep = jnp.where(one, 2.0, 0.0)
        sign = jnp.where(one, -1.0, 1.0)
        square_trace = jnp.zeros((1, 1), jnp.float32)
        if iteration < ITERS - 1:
            for t in range(tiles):
                ids = slice(t * tile, (t + 1) * tile)
                square = jnp.dot(b[now], b[now, :, ids], preferred_element_type=jnp.float32)
                square_trace = square_trace + diagonal_sum(square[ids, :], 0)
                fresh = keep * x[:, ids] + sign * square
                x[:, ids] = fresh
                b[later, :, ids] = fresh.astype(jnp.bfloat16)
        else:
            for t in range(tiles):
                ids = slice(t * tile, (t + 1) * tile)
                part = b[now, :, ids].astype(jnp.float32)
                square_trace = square_trace + jnp.sum(part * part, keepdims=True)
            square = jnp.dot(
                b[now, pl.ds(row_first, rows_here), :],
                b[now, :, pl.ds(col_first, cols_here)],
                preferred_element_type=jnp.float32,
            )
            mine = x[pl.ds(row_first, rows_here), pl.ds(col_first, cols_here)]
            density_ref[...] = keep * mine + sign * square
        records.append((trace, square_trace))
        trace = keep * trace + sign * square_trace
    shape = occupations_ref.shape
    row_ids = lax.broadcasted_iota(jnp.int32, shape, 0)
    col_ids = lax.broadcasted_iota(jnp.int32, shape, 1)
    out = jnp.zeros(shape, jnp.float32)
    for k, pair in enumerate(records):
        for j, value in enumerate(pair):
            out = jnp.where((row_ids == k) & (col_ids == j), value / size, out)
    occupations_ref[...] = out


def compute_kernel(rows_here, cols_here, branches, start, density_ref, occupations_ref, x, b):
    x[...] = start[...]
    purify(x, b, branches, rows_here, cols_here, density_ref, occupations_ref)


def body(density_start, branches):
    rows_here, cols_here = density_start.shape
    size = cols_here * lax.axis_size("col")
    whole = lax.all_gather(density_start, "col", axis=1, tiled=True)
    whole = lax.all_gather(whole, "row", axis=0, tiled=True)
    return pl.pallas_call(
        functools.partial(compute_kernel, rows_here, cols_here),
        out_shape=(
            jax.ShapeDtypeStruct((rows_here, cols_here), jnp.float32),
            jax.ShapeDtypeStruct((ITERS, 2), jnp.float32),
        ),
        in_specs=[
            pl.BlockSpec(memory_space=pltpu.SMEM),
            pl.BlockSpec(memory_space=pltpu.VMEM),
        ],
        out_specs=(
            pl.BlockSpec(memory_space=pltpu.VMEM),
            pl.BlockSpec(memory_space=pltpu.VMEM),
        ),
        scratch_shapes=[
            pltpu.VMEM((size, size), jnp.float32),
            pltpu.VMEM((2, size, size), jnp.bfloat16),
        ],
    )(branches, whole)


def solution(mesh):
    in_specs = (P("row", "col"), P())
    out_specs = (P("row", "col"), P())
    return jax.shard_map(body, mesh=mesh, in_specs=in_specs, out_specs=out_specs, check_vma=False)
```

time: 192 us -> 60.2 us (0.31)
  blocking collectives: 174 us -> 17 us
  waiting for transfers between devices: 0 us -> 23.5 us
  between operations: 4.56 us -> 14 us
  other arithmetic: 8.46 us -> 0 us
  Pallas kernels: 0 us -> 4.12 us
  matrix products: 2.26 us -> 0 us
    all_gather x12 -> x1, blocking collectives: 134 us -> 17 us  [body(): whole = lax.all_gather(density_start, 'col', axis=1, tiled=True)]
    psum x1 -> x0, blocking collectives: 39.5 us -> none  [body(): stacked = lax.psum(stacked, ('row', 'col'))]
    all_gather x0 -> x1, waiting for transfers between devices: none -> 23.5 us  [body(): whole = lax.all_gather(whole, 'row', axis=0, tiled=True)]
    another operation x6 -> x0, other arithmetic: 7.88 us -> none  [body(): stacked = jnp.stack(records)]
    pallas_call x0 -> x1, Pallas kernels: none -> 4.12 us  [body(): pl.pallas_call(functools.partial(compute_kernel, rows_here, cols_here), o...]
    dot_general x6 -> x0, matrix products: 2.26 us -> none  [add_rows(): jnp.dot(panel_part, shard_piece, preferred_element_type=jnp.float32)]
  transfers between devices with their start and end apart: 0 -> 1, of which waited for: 0 -> 1; matrix products, arithmetic and copies ran while one was open for 0% -> 0% of each run, Pallas kernels for 0% -> 0%
where the time goes in v1:
time: 60.2 us; the launch traced here: 59.9 us
  waiting for transfers between devices  23.5 us (39%)
  blocking collectives  17 us (28%)
  between operations  14 us (23%)
  Pallas kernels  4.12 us (7%)
  local copies, waits for them, and re-layouts  1.31 us (2%)
    all_gather x1, waiting for transfers between devices, body(): whole = lax.all_gather(whole, 'row', axis=0, tiled=True)  23.5 us
    all_gather x1, blocking collectives, body(): whole = lax.all_gather(density_start, 'col', axis=1, tiled=True)  17 us
    pallas_call x1, Pallas kernels, body(): pl.pallas_call(functools.partial(compute_kernel, rows_here, cols_here), o...  4.12 us
    pallas_call x1, local copies, waits for them, and re-layouts, body(): pl.pallas_call(functools.partial(compute_kernel, rows_here, cols_here), o...  1.31 us
  transfers between devices with their start and end apart: 1, of which 1 were waited for; matrix products, arithmetic and copies ran while one was open for 0% of the time, Pallas kernels for 0%

profile of v1, /device:TPU:0, one launch (start us, length us, event | category | flops | bytes accessed | tf_op | source)
XLA Modules:
  0.0 59.9 jit_solution(11048582159950367619)
XLA Ops:
  7.2 0.0 all-gather.2.cloned.1.call-start
  7.2 17.0 %all_gather.6 = f32[64,512]{1,0:T(8,128)} all-gather(f32[64,128]{1,0:T(8,128)} %param.2), channel_id=1, replica_groups=mesh['row'=8,'col'=4] {'col'}, dimensions={1}, use_global_device_ids=true | all-gather | bytes 163840 | tf_op jit(solution)/shard_map/all_gather | solution.py:78
  24.2 0.0 all-gather.2.cloned.1.call-update
  24.2 23.5 %all-gather.2.cloned.1.call-done.start = f32[512,512]{1,0:T(8,128)} async-done(((f32[64,512]{1,0:T(8,128)}), f32[512,512]{1,0:T(8,128)}) %all-gather.2.cloned.1.call-update) | async-done | bytes 1048592 | tf_op jit(solution)/shard_map/all_gather | solution.py:79
  47.6 4.1 %shard_map.41 = (f32[64,128]{1,0:T(8,128)}, f32[6,2]{1,0:T(8,128)}) custom-call(s32[6]{0:T(128)} %branches.1, f32[512,512]{1,0:T(8,128)} %all-gather.2.cloned.1.call-done.start), custom_call_target="tpu_custom_call" | custom-call | tf_op jit(solution)/shard_map/pallas_call | solution.py:80
  51.8 1.3 %copy.4 = f32[6,2]{0,1:T(2,128)} copy(f32[6,2]{1,0:T(8,128)} %get-tuple-element.3) | data formatting | bytes 96 | tf_op jit(solution)/shard_map/pallas_call | solution.py:80
Async XLA Ops:
  7.2 40.5 %all-gather.2.cloned.1.call-start = ((), (), s32[]{:S(2)}) async-start(), calls=%async_computation | async-start | bytes 1179648 | tf_op jit(solution)/shard_map/all_gather | solution.py:79
Sparse Core Ops, SparseCore 0:
  24.3 23.2 all-gather.1

commit v2 on v1

--- a/solution.py
+++ b/solution.py
@@ -66,26 +66,131 @@
             out = jnp.where((row_ids == k) & (col_ids == j), value / size, out)
     occupations_ref[...] = out
 
-
-def compute_kernel(rows_here, cols_here, branches, start, density_ref, occupations_ref, x, b):
-    x[...] = start[...]
+MESH = pl.DeviceIdType.MESH
+
+
+def xor_fixed(index, bits, fixed):
+    out = 0
+    for bit in range(bits):
+        digit = lax.rem(lax.div(index, 1 << bit), 2)
+        out = out + ((1 - digit) if (fixed >> bit) & 1 else digit) * (1 << bit)
+    return out
+
+
+def xor_traced(left, right, bits):
+    out = 0
+    for bit in range(bits):
+        a = lax.rem(lax.div(left, 1 << bit), 2)
+        b = lax.rem(lax.div(right, 1 << bit), 2)
+        out = out + (a + b - 2 * a * b) * (1 << bit)
+    return out
+
+
+def relay_slots(tiles):
+    slots = [(d, 0) for d in range(1, tiles)]
+    for a in range(1, tiles):
+        for b in range(a + 1, tiles):
+            d = min((bin(v).count("1"), v) for v in (a, b))[1]
+            slots.append((d, a ^ b))
+    return slots
+
+
+def whole_kernel(tiles, halves, slots, branches, start, density_ref, occupations_ref,
+                 x, b, local_sem, line_send, line_recv, relay_send, relay_recv, peer_send, peer_recv):
+    rows_here, cols_here = density_ref.shape
+    bits = tiles.bit_length() - 1
+    row, col = lax.axis_index("row"), lax.axis_index("col")
+    band, half = lax.div(row, halves), lax.rem(row, halves)
+
+    def block(band_at, col_at):
+        first = pl.multiple_of((band_at * halves + half) * rows_here, rows_here)
+        return x.at[pl.ds(first, rows_here), pl.ds(pl.multiple_of(col_at * cols_here, cols_here), cols_here)]
+
+    def tile(band_at, col_at):
+        side = cols_here
+        return (pl.ds(pl.multiple_of(band_at * side, side), side),
+                pl.ds(pl.multiple_of(col_at * side, side), side))
+
+    own = pltpu.make_async_copy(start, block(band, col), local_sem)
+    own.start()
+
+    cols = [xor_fixed(col, bits, k) for k in range(tiles)]
+    bands = [xor_fixed(band, bits, d) for d in range(tiles)]
+    peers = [band * halves + lax.rem(half + s, halves) for s in range(1, halves)]
+    partners = [(row, cols[k]) for k in range(1, tiles)]
+    partners += [(bands[d] * halves + half, col) for d in range(1, tiles)]
+    partners += [(p, col) for p in peers]
+    barrier = pltpu.get_barrier_semaphore()
+    for partner in partners:
+        pl.semaphore_signal(barrier, inc=1, device_id=partner, device_id_type=MESH)
+    pl.semaphore_wait(barrier, len(partners))
+    own.wait()
+
+    def send(ref, send_sem, recv_sem, device):
+        return pltpu.make_async_remote_copy(
+            src_ref=ref, dst_ref=ref, send_sem=send_sem, recv_sem=recv_sem,
+            device_id=device, device_id_type=MESH,
+        )
+
+    line = {k: send(block(band, col), line_send.at[k], line_recv.at[k], (row, cols[k]))
+            for k in range(1, tiles)}
+    relay = [send(block(band, bands[e]), relay_send.at[i], relay_recv.at[i], (bands[d] * halves + half, col))
+             for i, (d, e) in enumerate(slots)]
+    held = [block(band, cols[k]) for k in range(tiles)]
+    held += [block(bands[d], bands[d ^ e]) for d, e in slots]
+    peer = [[send(ref, peer_send.at[s, i], peer_recv.at[s, i], (p, col)) for s, p in enumerate(peers)]
+            for i, ref in enumerate(held)]
+
+    for k in range(1, tiles):
+        line[k].start()
+    for k in range(tiles):
+        if k:
+            line[k].wait_recv()
+        here = xor_traced(band, cols[k], bits)
+        for e in range(tiles):
+            @pl.when(here == e)
+            def _():
+                for i, slot in enumerate(slots):
+                    if slot[1] == e:
+                        relay[i].start()
+        for copy in peer[k]:
+            copy.start()
+    for i in range(len(slots)):
+        relay[i].wait_recv()
+        for copy in peer[tiles + i]:
+            copy.start()
+    for k in range(tiles):
+        for copy in peer[k]:
+            copy.wait_recv()
+    for e in range(1, tiles):
+        x[tile(bands[e], band)] = x[tile(band, bands[e])].T
+    for i, (d, e) in enumerate(slots):
+        for copy in peer[tiles + i]:
+            copy.wait_recv()
+        if e:
+            x[tile(bands[d ^ e], bands[d])] = x[tile(bands[d], bands[d ^ e])].T
+    for copy in list(line.values()) + relay + [c for group in peer for c in group]:
+        copy.wait_send()
     purify(x, b, branches, rows_here, cols_here, density_ref, occupations_ref)
 
 
 def body(density_start, branches):
     rows_here, cols_here = density_start.shape
-    size = cols_here * lax.axis_size("col")
-    whole = lax.all_gather(density_start, "col", axis=1, tiled=True)
-    whole = lax.all_gather(whole, "row", axis=0, tiled=True)
+    tiles = lax.axis_size("col")
+    halves = lax.axis_size("row") // tiles
+    assert tiles & (tiles - 1) == 0 and halves * rows_here == cols_here
+    size = cols_here * tiles
+    slots = relay_slots(tiles)
+    dma = pltpu.SemaphoreType.DMA
     return pl.pallas_call(
-        functools.partial(compute_kernel, rows_here, cols_here),
+        functools.partial(whole_kernel, tiles, halves, slots),
         out_shape=(
             jax.ShapeDtypeStruct((rows_here, cols_here), jnp.float32),
             jax.ShapeDtypeStruct((ITERS, 2), jnp.float32),
         ),
         in_specs=[
             pl.BlockSpec(memory_space=pltpu.SMEM),
-            pl.BlockSpec(memory_space=pltpu.VMEM),
+            pl.BlockSpec(memory_space=pl.ANY),
         ],
         out_specs=(
             pl.BlockSpec(memory_space=pltpu.VMEM),
@@ -94,8 +199,16 @@
         scratch_shapes=[
             pltpu.VMEM((size, size), jnp.float32),
             pltpu.VMEM((2, size, size), jnp.bfloat16),
+            dma,
+            dma((tiles,)),
+            dma((tiles,)),
+            dma((len(slots),)),
+            dma((len(slots),)),
+            dma((halves - 1, tiles + len(slots))),
+            dma((halves - 1, tiles + len(slots))),
         ],
-    )(branches, whole)
+        compiler_params=pltpu.CompilerParams(collective_id=0, has_side_effects=True),
+    )(branches, density_start)
 
 
 def solution(mesh):

time: 60.2 us -> 22.1 us (0.37)
  waiting for transfers between devices: 23.5 us -> 0 us
  blocking collectives: 17 us -> 0 us
  Pallas kernels: 4.12 us -> 18.4 us
  between operations: 14 us -> 0.64 us
  local copies, waits for them, and re-layouts: 1.31 us -> 2.7 us
    all_gather x1 -> x0, waiting for transfers between devices: 23.5 us -> none  [body(): whole = lax.all_gather(whole, 'row', axis=0, tiled=True)]
    all_gather x1 -> x0, blocking collectives: 17 us -> none  [body(): whole = lax.all_gather(density_start, 'col', axis=1, tiled=True)]
    pallas_call x1, Pallas kernels: 4.12 us -> 18.4 us  [body(): pl.pallas_call(functools.partial(whole_kernel, tiles, halves, slots), out...]
    unnamed x0 -> x1, local copies, waits for them, and re-layouts: none -> 1.37 us
  transfers between devices with their start and end apart: 1 -> 0, of which waited for: 1 -> 0; matrix products, arithmetic and copies ran while one was open for 0% -> 0% of each run, Pallas kernels for 0% -> 0%
where the time goes in v2:
time: 22.1 us; the launch traced here: 21.7 us
  Pallas kernels  18.4 us (83%)
  local copies, waits for them, and re-layouts  2.7 us (12%)
  between operations  0.64 us (3%)
    pallas_call x1, Pallas kernels, body(): pl.pallas_call(functools.partial(whole_kernel, tiles, halves, slots), out...  18.4 us
    unnamed x1, local copies, waits for them, and re-layouts  1.37 us
    pallas_call x1, local copies, waits for them, and re-layouts, body(): pl.pallas_call(functools.partial(whole_kernel, tiles, halves, slots), out...  1.32 us

profile of v2, /device:TPU:0, one launch (start us, length us, event | category | flops | bytes accessed | tf_op | source)
XLA Modules:
  0.0 21.7 jit_solution(5204731379327376073)
XLA Ops:
  0.6 18.4 %shard_map.41 = (f32[64,128]{1,0:T(8,128)}, f32[6,2]{1,0:T(8,128)}) custom-call(s32[6]{0:T(128)} %branches.1, f32[64,128]{1,0:T(8,128)} %start.1), custom_call_target="tpu_custom_call" | custom-call | tf_op jit(solution)/shard_map/pallas_call | solution.py:185
  19.0 1.3 %copy.4 = f32[6,2]{0,1:T(2,128)} copy(f32[6,2]{1,0:T(8,128)} %get-tuple-element.3) | data formatting | bytes 96 | tf_op jit(solution)/shard_map/pallas_call | solution.py:185
  20.3 1.4 %copy.6 = f32[64,128]{1,0:T(8,128)} copy(f32[64,128]{1,0:T(8,128)} %get-tuple-element.6) | data formatting | bytes 65536
